TPU v7x, 32 devices: a whole 2x2x4 slice. The times are simulated.
32 devices in a mesh: wide: 8 (over y, x, core), narrow: 4 (over z).
Axes of the slice: x: 2, y: 2, z: 4, core: 2. Of those that a mesh axis runs over, the one named last changes fastest.
Arguments:
- tokens: bfloat16 [65536, 768], P(('wide', 'narrow')), may hold values from -6 to 6
- cotangent: bfloat16 [65536, 768], P(('wide', 'narrow')), may hold values from -6 to 6
- segment_ids: int32 [128, 512], P(('wide', 'narrow')), may hold values from 0 to 3, never falling along the last dimension, each value on 1 to 256 neighbouring positions
- feature_ids: int32 [128, 512], P(('wide', 'narrow')), may hold values from 0 to 15
- attention_master: float32 [3072, 768], P(('wide', 'narrow')), may hold values from -1.1547005 to 1.1547005
- attention_first: float32 [3072, 768], P(('wide', 'narrow')), may hold values from -1024 to 1024
- attention_second: float32 [3072, 768], P(('wide', 'narrow')), may hold values from 327.68 to 262144
- feedforward_master: float32 [6144, 768], P(('wide', 'narrow')), may hold values from -0.14433757 to 0.14433757
- feedforward_first: float32 [6144, 768], P(('wide', 'narrow')), may hold values from -1024 to 1024
- feedforward_second: float32 [6144, 768], P(('wide', 'narrow')), may hold values from 327.68 to 262144
- vector_master: float32 [13, 768], P(None, ('wide', 'narrow')), may hold values from -0.8 to 1.5
- vector_first: float32 [13, 768], P(None, ('wide', 'narrow')), may hold values from -1024 to 1024
- vector_second: float32 [13, 768], P(None, ('wide', 'narrow')), may hold values from 327.68 to 262144
Outputs:
- block_out: bfloat16 [65536, 768], P(('wide', 'narrow'))
- tokens_grad: bfloat16 [65536, 768], P(('wide', 'narrow'))
- attention_master_new: float32 [3072, 768], P(('wide', 'narrow'))
- attention_first_new: float32 [3072, 768], P(('wide', 'narrow'))
- attention_second_new: float32 [3072, 768], P(('wide', 'narrow'))
- attention_copy: bfloat16 [3072, 768], P(('wide', 'narrow'))
- feedforward_master_new: float32 [6144, 768], P(('wide', 'narrow'))
- feedforward_first_new: float32 [6144, 768], P(('wide', 'narrow'))
- feedforward_second_new: float32 [6144, 768], P(('wide', 'narrow'))
- feedforward_copy: bfloat16 [6144, 768], P(('wide', 'narrow'))
- vector_master_new: float32 [13, 768], P(None, ('wide', 'narrow'))
- vector_first_new: float32 [13, 768], P(None, ('wide', 'narrow'))
- vector_second_new: float32 [13, 768], P(None, ('wide', 'narrow'))
- vector_copy: bfloat16 [13, 768], P(None, ('wide', 'narrow'))
All inputs are finite; a program needn't handle non-finite values.
Results may differ from a plain program's by a relative error of at most 0.015.
The roundings to bfloat16 on the way count: a program that leaves them out, or rounds other values in their place, can miss the bound.
Values may be sent and summed in bfloat16 or wider, within the bound.
A program may use at most 256 MiB of HBM per device.

v0:
```python
from functools import partial

import jax
import jax.numpy as jnp
from jax import lax
from jax.sharding import PartitionSpec as P

D = 768
FF = 3072
HEADS = 12
HEAD_DIM = 64
ADAM_STEP = 3


NORM_EPS = 1e-05
BETA = 0.5
ADAM_EPS = 1e-08
DECAY = 0.01
VECTOR_RATE = 0.1
MASKED = -1000000000.0


def layer_norm(summed, gain_row, shift_row):
    average = jnp.mean(summed, axis=-1, keepdims=True)
    centred = summed - average
    variance = jnp.mean(centred * centred, axis=-1, keepdims=True)
    return centred * lax.rsqrt(variance + NORM_EPS) * gain_row + shift_row


def group_matrix(segment_row, feature_row):
    same_segment = segment_row[:, None] == segment_row[None, :]
    return same_segment & (feature_row[:, None] == feature_row[None, :])


def masked_scores(queries, key_rows, segment_row):
    length = queries.shape[0]
    scores = jnp.einsum(
        "qhd,khd->hqk",
        queries.reshape(length, HEADS, HEAD_DIM),
        key_rows.reshape(length, HEADS, HEAD_DIM),
        preferred_element_type=jnp.float32,
    )
    allowed = segment_row[:, None] == segment_row[None, :]
    return jnp.where(allowed[None], scores, MASKED)


def contract_rows(left, right):
    return lax.dot_general(
        left, right, (((0,), (0,)), ((), ())), preferred_element_type=jnp.float32
    )


def contract_cols(left, right):
    return lax.dot_general(
        left, right, (((1,), (1,)), ((), ())), preferred_element_type=jnp.float32
    )


def forward_sequence(
    token_rows, segment_row, feature_row, attention_all, feedforward_all, vector_float
):
    expand = FF // D
    length = token_rows.shape[0]
    same_group = group_matrix(segment_row, feature_row)
    members = jnp.sum(same_group.astype(jnp.float32), axis=1, keepdims=True)
    merging = (
        jnp.dot(same_group.astype(jnp.bfloat16), token_rows, preferred_element_type=jnp.float32)
        / members
    )
    mixed = token_rows.astype(jnp.float32) + vector_float[0] * merging
    rounded_in = mixed.astype(jnp.bfloat16)
    projected = jnp.einsum(
        "td,jde->jte",
        rounded_in,
        attention_all[: 3 * D].reshape(3, D, D),
        preferred_element_type=jnp.float32,
    )
    queries = ((projected[0] + vector_float[1]) * 0.125).astype(jnp.bfloat16)
    key_rows = projected[1].astype(jnp.bfloat16)
    values = (projected[2] + vector_float[2]).astype(jnp.bfloat16)
    scores = masked_scores(queries, key_rows, segment_row)
    highest = jnp.max(scores, axis=-1, keepdims=True)
    exponent = jnp.exp(scores - highest)
    totals = jnp.sum(exponent, axis=-1, keepdims=True)
    attention = exponent / totals
    logsum = highest + jnp.log(totals)
    context = jnp.einsum(
        "hqk,khd->qhd",
        attention.astype(jnp.bfloat16),
        values.reshape(length, HEADS, HEAD_DIM),
        preferred_element_type=jnp.float32,
    )
    context = context.reshape(length, D).astype(jnp.bfloat16)
    first_sum = (
        mixed
        + jnp.dot(context, attention_all[3 * D :], preferred_element_type=jnp.float32)
        + vector_float[3]
    )
    normed = layer_norm(first_sum, vector_float[4], vector_float[5])
    hidden_pre = contract_cols(normed.astype(jnp.bfloat16), feedforward_all[:FF]) + vector_float[
        6 : 6 + expand
    ].reshape(FF)
    activated = jax.nn.gelu(hidden_pre, approximate=False).astype(jnp.bfloat16)
    second_sum = (
        normed
        + jnp.dot(activated, feedforward_all[FF:], preferred_element_type=jnp.float32)
        + vector_float[6 + expand]
    )
    output = layer_norm(second_sum, vector_float[7 + expand], vector_float[8 + expand])
    stored = (
        merging,
        mixed,
        queries,
        key_rows,
        values,
        logsum,
        context,
        first_sum,
        hidden_pre,
        second_sum,
    )
    return (output.astype(jnp.bfloat16), stored)


def feedforward_backward(stored, grad_rows, feedforward_all, vector_float):
    expand = FF // D
    (
        merging,
        mixed,
        queries,
        key_rows,
        values,
        logsum,
        context,
        first_sum,
        hidden_pre,
        second_sum,
    ) = stored
    normed, early_pull = jax.vjp(layer_norm, first_sum, vector_float[4], vector_float[5])
    _, late_pull = jax.vjp(
        layer_norm, second_sum, vector_float[7 + expand], vector_float[8 + expand]
    )
    grad_second, late_gain, late_shift = late_pull(grad_rows.astype(jnp.float32))
    branch_grad = grad_second.astype(jnp.bfloat16)
    activated = jax.nn.gelu(hidden_pre, approximate=False).astype(jnp.bfloat16)
    down_grad = contract_rows(activated, branch_grad)
    activated_grad = contract_cols(branch_grad, feedforward_all[FF:])
    _, gelu_pull = jax.vjp(partial(jax.nn.gelu, approximate=False), hidden_pre)
    hidden_grad = gelu_pull(activated_grad)[0].astype(jnp.bfloat16)
    up_grad = contract_rows(hidden_grad, normed.astype(jnp.bfloat16))
    normed_grad = grad_second + jnp.dot(
        hidden_grad, feedforward_all[:FF], preferred_element_type=jnp.float32
    )
    first_grad, early_gain, early_shift = early_pull(normed_grad)
    vector_part = jnp.concatenate(
        [
            early_gain[None],
            early_shift[None],
            jnp.sum(hidden_grad.astype(jnp.float32), axis=0).reshape(expand, D),
            jnp.sum(grad_second, axis=0)[None],
            late_gain[None],
            late_shift[None],
        ],
        axis=0,
    )
    return (first_grad, jnp.concatenate([up_grad, down_grad], axis=0), vector_part)


def attention_backward(
    stored, first_grad, token_rows, segment_row, feature_row, attention_all, vector_float
):
    (
        merging,
        mixed,
        queries,
        key_rows,
        values,
        logsum,
        context,
        first_sum,
        hidden_pre,
        second_sum,
    ) = stored
    length = token_rows.shape[0]
    branch_grad = first_grad.astype(jnp.bfloat16)
    output_grad = contract_rows(context, branch_grad)
    context_grad = (
        contract_cols(branch_grad, attention_all[3 * D :])
        .astype(jnp.bfloat16)
        .reshape(length, HEADS, HEAD_DIM)
    )
    attention = jnp.exp(masked_scores(queries, key_rows, segment_row) - logsum)
    query_heads = queries.reshape(length, HEADS, HEAD_DIM)
    key_heads = key_rows.reshape(length, HEADS, HEAD_DIM)
    value_heads = values.reshape(length, HEADS, HEAD_DIM)
    value_grad = jnp.einsum(
        "hqk,qhd->khd",
        attention.astype(jnp.bfloat16),
        context_grad,
        preferred_element_type=jnp.float32,
    )
    value_grad = value_grad.reshape(length, D).astype(jnp.bfloat16)
    prob_grad = jnp.einsum(
        "qhd,khd->hqk", context_grad, value_heads, preferred_element_type=jnp.float32
    )
    row_dot = jnp.sum(attention * prob_grad, axis=-1, keepdims=True)
    score_grad = (attention * (prob_grad - row_dot)).astype(jnp.bfloat16)
    query_grad = jnp.einsum(
        "hqk,khd->qhd", score_grad, key_heads, preferred_element_type=jnp.float32
    )
    query_grad = query_grad.reshape(length, D).astype(jnp.bfloat16) * 0.125
    key_grad = jnp.einsum(
        "hqk,qhd->khd", score_grad, query_heads, preferred_element_type=jnp.float32
    )
    key_grad = key_grad.reshape(length, D).astype(jnp.bfloat16)
    stacked = jnp.stack([query_grad, key_grad, value_grad])
    rounded_in = mixed.astype(jnp.bfloat16)
    project_grad = jnp.einsum(
        "td,jte->jde", rounded_in, stacked, preferred_element_type=jnp.float32
    ).reshape(3 * D, D)
    mixed_grad = first_grad + jnp.einsum(
        "jte,jde->td",
        stacked,
        attention_all[: 3 * D].reshape(3, D, D),
        preferred_element_type=jnp.float32,
    )
    same_group = group_matrix(segment_row, feature_row)
    members = jnp.sum(same_group.astype(jnp.float32), axis=1, keepdims=True)
    spread = (vector_float[0] * mixed_grad / members).astype(jnp.bfloat16)
    tokens_grad = mixed_grad + jnp.dot(
        same_group.astype(jnp.bfloat16), spread, preferred_element_type=jnp.float32
    )
    vector_part = jnp.stack(
        [
            jnp.sum(mixed_grad * merging, axis=0),
            jnp.sum(query_grad.astype(jnp.float32), axis=0),
            jnp.sum(value_grad.astype(jnp.float32), axis=0),
            jnp.sum(first_grad, axis=0),
        ]
    )
    return (tokens_grad, jnp.concatenate([project_grad, output_grad], axis=0), vector_part)


def adam_step(master, first, second, gradient, rate):
    first_new = BETA * first + (1.0 - BETA) * gradient
    second_new = BETA * second + (1.0 - BETA) * gradient * gradient
    correction = 1.0 - BETA**ADAM_STEP
    master_new = master - rate * (
        first_new / correction / (jnp.sqrt(second_new / correction) + ADAM_EPS) + DECAY * master
    )
    return (master_new, first_new, second_new)


def local(
    tokens,
    cotangent,
    segment_ids,
    feature_ids,
    attention_master,
    attention_first,
    attention_second,
    feedforward_master,
    feedforward_first,
    feedforward_second,
    vector_master,
    vector_first,
    vector_second,
):
    expand = FF // D
    seqs_here = segment_ids.shape[0]
    length = segment_ids.shape[1]
    attention_all, feedforward_all, vector_all = (
        lax.all_gather(
            attention_master.astype(jnp.bfloat16), ("wide", "narrow"), axis=0, tiled=True
        ),
        lax.all_gather(
            feedforward_master.astype(jnp.bfloat16), ("wide", "narrow"), axis=0, tiled=True
        ),
        lax.all_gather(vector_master.astype(jnp.bfloat16), ("wide", "narrow"), axis=1, tiled=True),
    )
    token_blocks = tokens.reshape(seqs_here, length, D)
    grad_blocks = cotangent.reshape(seqs_here, length, D)
    vector_float = vector_all.astype(jnp.float32)

    def run_forward(inputs):
        token_rows, segment_row, feature_row = inputs
        return forward_sequence(
            token_rows, segment_row, feature_row, attention_all, feedforward_all, vector_float
        )

    outputs, stored = lax.map(run_forward, (token_blocks, segment_ids, feature_ids))
    attention_back, feedforward_back, vector_back = (
        lax.all_gather(
            attention_master.astype(jnp.bfloat16), ("wide", "narrow"), axis=0, tiled=True
        ),
        lax.all_gather(
            feedforward_master.astype(jnp.bfloat16), ("wide", "narrow"), axis=0, tiled=True
        ),
        lax.all_gather(vector_master.astype(jnp.bfloat16), ("wide", "narrow"), axis=1, tiled=True),
    )
    vector_back_float = vector_back.astype(jnp.float32)

    def feedforward_turn(running, inputs):
        stored_seq, grad_rows = inputs
        first_grad, weight_part, vector_part = feedforward_backward(
            stored_seq, grad_rows, feedforward_back, vector_back_float
        )
        return ((running[0] + weight_part, running[1] + vector_part), first_grad)

    start_late = (jnp.zeros((2 * FF, D), jnp.float32), jnp.zeros((5 + expand, D), jnp.float32))
    (feedforward_grad, late_vector), first_grads = lax.scan(
        feedforward_turn, start_late, (stored, grad_blocks)
    )

    def attention_turn(running, inputs):
        stored_seq, first_grad, token_rows, segment_row, feature_row = inputs
        tokens_grad, weight_part, vector_part = attention_backward(
            stored_seq,
            first_grad,
            token_rows,
            segment_row,
            feature_row,
            attention_back,
            vector_back_float,
        )
        return ((running[0] + weight_part, running[1] + vector_part), tokens_grad)

    start_early = (jnp.zeros((4 * D, D), jnp.float32), jnp.zeros((4, D), jnp.float32))
    (attention_grad, early_vector), token_grads = lax.scan(
        attention_turn, start_early, (stored, first_grads, token_blocks, segment_ids, feature_ids)
    )
    vector_grad = jnp.concatenate([early_vector, late_vector], axis=0)
    attention_owned, feedforward_owned, vector_owned = (
        lax.psum_scatter(attention_grad, ("wide", "narrow"), scatter_dimension=0, tiled=True),
        lax.psum_scatter(feedforward_grad, ("wide", "narrow"), scatter_dimension=0, tiled=True),
        lax.psum_scatter(vector_grad, ("wide", "narrow"), scatter_dimension=1, tiled=True),
    )
    device = lax.axis_index(("wide", "narrow"))
    attention_rows = attention_master.shape[0]
    attention_index = (device * attention_rows + jnp.arange(attention_rows))[:, None]
    attention_rate = jnp.where(attention_index < 3 * D, D ** (-0.5), (D // 64) ** (-0.5))
    feedforward_rows = feedforward_master.shape[0]
    feedforward_index = (device * feedforward_rows + jnp.arange(feedforward_rows))[:, None]
    feedforward_rate = jnp.where(feedforward_index < FF, D ** (-0.5), FF ** (-0.5))
    attention_new, attention_first_new, attention_second_new = adam_step(
        attention_master, attention_first, attention_second, attention_owned, attention_rate
    )
    feedforward_new, feedforward_first_new, feedforward_second_new = adam_step(
        feedforward_master,
        feedforward_first,
        feedforward_second,
        feedforward_owned,
        feedforward_rate,
    )
    vector_new, vector_first_new, vector_second_new = adam_step(
        vector_master, vector_first, vector_second, vector_owned, VECTOR_RATE
    )
    return (
        outputs.reshape(seqs_here * length, D),
        token_grads.reshape(seqs_here * length, D).astype(jnp.bfloat16),
        attention_new,
        attention_first_new,
        attention_second_new,
        attention_new.astype(jnp.bfloat16),
        feedforward_new,
        feedforward_first_new,
        feedforward_second_new,
        feedforward_new.astype(jnp.bfloat16),
        vector_new,
        vector_first_new,
        vector_second_new,
        vector_new.astype(jnp.bfloat16),
    )


def solution(mesh):
    placed = (
        P(("wide", "narrow"), None),
        P(("wide", "narrow"), None),
        P(("wide", "narrow"), None),
        P(("wide", "narrow"), None),
        P(("wide", "narrow"), None),
        P(("wide", "narrow"), None),
        P(("wide", "narrow"), None),
        P(("wide", "narrow"), None),
        P(("wide", "narrow"), None),
        P(("wide", "narrow"), None),
        P(None, ("wide", "narrow")),
        P(None, ("wide", "narrow")),
        P(None, ("wide", "narrow")),
    )
    return jax.shard_map(
        local,
        mesh=mesh,
        in_specs=placed,
        out_specs=(
            P(("wide", "narrow"), None),
            P(("wide", "narrow"), None),
            P(("wide", "narrow"), None),
            P(("wide", "narrow"), None),
            P(("wide", "narrow"), None),
            P(("wide", "narrow"), None),
            P(("wide", "narrow"), None),
            P(("wide", "narrow"), None),
            P(("wide", "narrow"), None),
            P(("wide", "narrow"), None),
            P(None, ("wide", "narrow")),
            P(None, ("wide", "narrow")),
            P(None, ("wide", "narrow")),
            P(None, ("wide", "narrow")),
        ),
        check_vma=False,
    )
```

profile of v0, /device:TPU:0, one launch (start us, length us, event | category | flops | bytes accessed | tf_op | source)
XLA Modules:
  0.0 1471.0 jit_solution(15119482238642646173)
XLA Ops:
  11.6 71.6 %all-gather = bf16[32,24,13]{1,2,0:T(8,128)(2,1)S(1)} all-gather(bf16[1,24,13]{1,2,0:T(8,128)(2,1)S(1)} %convert_bitcast_fusion.1), channel_id=1, replica_groups=mesh['wide'=8,'narrow'=4] {'wide','narrow'}, dimensions={0}, use_global_device_ids=true | all-gather | bytes 20592 | tf_op jit(solution)/shard_map/all_gather | solution.py:279
  89.4 71.8 %all-gather.6.cloned.1.call-done = bf16[6144,768]{1,0:T(8,128)(2,1)} async-done(((bf16[192,768]{1,0:T(8,128)(2,1)}), bf16[6144,768]{1,0:T(8,128)(2,1)}) %all-gather.6.cloned.1.call-update) | async-done | bytes 9437200 | tf_op jit(solution)/shard_map/all_gather | solution.py:276
  170.8 294.5 %while.60 = (s32[]{:T(128)}, bf16[4,512,768]{2,1,0:T(8,128)(2,1)}, f32[4,512,768]{2,1,0:T(8,128)}, bf16[4,512,768]{2,1,0:T(8,128)(2,1)}, bf16[4,512,768]{2,1,0:T...) while((s32[]{:T(128)}, bf16[4,512,768]{2,1,0:T(8,128)(2,1)}, ...), condition=%wide.region_8.9_spmd, body=%wide.region_0.8_spmd.sunk | while | flops 8610638848 | bytes 237444464 | solution.py:291
  236.7 18.3 %fusion.348 = (f32[512]{0:T(512)S(1)}, f32[512,768]{1,0:T(8,128)S(1)}) fusion(f32[768]{0:T(1024)S(1)} %get-tuple-element.952, bf16[6144,768]{1,0:T(8,128)(2,1)} %get-tuple-element.1092, f32[512,3072]{1,0:T(8,128)S(1)} %get-tuple-element.967, f32[3072]{0:T(1024)S(1)} %add.502, f32[768]{0:T(1024)S(1)} %get-tuple-element.964, ...), kind=kOutput, calls=%fused_computation.405.clone.1 | convolution fusion | flops 2522480128 | bytes 14183424 | tf_op jit(solution)/shard_map/while/body/eval_jaxpr/dot_general | solution.py:106
  305.1 18.3 %fusion.348 = (f32[512]{0:T(512)S(1)}, f32[512,768]{1,0:T(8,128)S(1)}) fusion(f32[768]{0:T(1024)S(1)} %get-tuple-element.952, bf16[6144,768]{1,0:T(8,128)(2,1)} %get-tuple-element.1092, f32[512,3072]{1,0:T(8,128)S(1)} %get-tuple-element.967, f32[3072]{0:T(1024)S(1)} %add.502, f32[768]{0:T(1024)S(1)} %get-tuple-element.964, ...), kind=kOutput, calls=%fused_computation.405.clone.1 | convolution fusion | flops 2522480128 | bytes 14183424 | tf_op jit(solution)/shard_map/while/body/eval_jaxpr/dot_general | solution.py:106
  373.5 18.3 %fusion.348 = (f32[512]{0:T(512)S(1)}, f32[512,768]{1,0:T(8,128)S(1)}) fusion(f32[768]{0:T(1024)S(1)} %get-tuple-element.952, bf16[6144,768]{1,0:T(8,128)(2,1)} %get-tuple-element.1092, f32[512,3072]{1,0:T(8,128)S(1)} %get-tuple-element.967, f32[3072]{0:T(1024)S(1)} %add.502, f32[768]{0:T(1024)S(1)} %get-tuple-element.964, ...), kind=kOutput, calls=%fused_computation.405.clone.1 | convolution fusion | flops 2522480128 | bytes 14183424 | tf_op jit(solution)/shard_map/while/body/eval_jaxpr/dot_general | solution.py:106
  442.0 18.3 %fusion.348 = (f32[512]{0:T(512)S(1)}, f32[512,768]{1,0:T(8,128)S(1)}) fusion(f32[768]{0:T(1024)S(1)} %get-tuple-element.952, bf16[6144,768]{1,0:T(8,128)(2,1)} %get-tuple-element.1092, f32[512,3072]{1,0:T(8,128)S(1)} %get-tuple-element.967, f32[3072]{0:T(1024)S(1)} %add.502, f32[768]{0:T(1024)S(1)} %get-tuple-element.964, ...), kind=kOutput, calls=%fused_computation.405.clone.1 | convolution fusion | flops 2522480128 | bytes 14183424 | tf_op jit(solution)/shard_map/while/body/eval_jaxpr/dot_general | solution.py:106
  468.5 338.3 %while.61 = (s32[]{:T(128)}, f32[6144,768]{1,0:T(8,128)}, f32[9,768]{1,0:T(8,128)S(1)}, f32[4,512,768]{2,1,0:T(8,128)}, f32[4,512,3072]{2,1,0:T(8,128)}, /*index...) while((s32[]{:T(128)}, f32[6144,768]{1,0:T(8,128)}, ...), condition=%wide.region_24.25_spmd.clone, body=%wide.region_9.24_spmd.clone.sunk | while | flops 9920854016 | bytes 209873232 | solution.py:311
  498.5 18.4 %convert_reduce_fusion.13 = (f32[3072]{0:T(1024)S(1)}, bf16[512,3072]{1,0:T(8,128)(2,1)S(1)}) fusion(bf16[6144,768]{1,0:T(8,128)(2,1)S(1)} %copy-done.20, f32[512,768]{1,0:T(8,128)S(1)} %get-tuple-element.993, f32[512]{0:T(512)S(1)} %negate_multiply_fusion.6, f32[4,512,3072]{2,1,0:T(8,128)} %get-tuple-element.1122, s32[]{:T(128)} %get-tuple-element.1106), kind=kOutput, calls=%fused_computation.177.clone.1 | convolution fusion | flops 2533094400 | bytes 15742980 | tf_op jit(solution)/shard_map/while/body/eval_jaxpr/dot_general | solution.py:54
  529.2 19.1 %fusion.357 = f32[3072,768]{1,0:T(8,128)S(1)} fusion(f32[4,512,3072]{2,1,0:T(8,128)} %get-tuple-element.1122, s32[]{:T(128)} %get-tuple-element.1106, f32[4,512,768]{2,1,0:T(8,128)} %get-tuple-element.1125, f32[512]{0:T(512)S(1)} %negate_multiply_fusion.6, f32[512]{0:T(512)S(1)} %multiply_multiply_fusion.17, f32[512]{0:T(512)S(1)} %broadcast_multiply_fusion.10, ...), kind=kOutput, calls=%fused_computation.208.clone.1 | convolution fusion | flops 2521694208 | bytes 18100224 | tf_op jit(solution)/shard_map/while/body/eval_jaxpr/dot_general | solution.py:48
  548.3 11.9 maximum_add_fusion.6
  568.8 18.4 %convert_reduce_fusion.13 = (f32[3072]{0:T(1024)S(1)}, bf16[512,3072]{1,0:T(8,128)(2,1)S(1)}) fusion(bf16[6144,768]{1,0:T(8,128)(2,1)S(1)} %copy-done.20, f32[512,768]{1,0:T(8,128)S(1)} %get-tuple-element.993, f32[512]{0:T(512)S(1)} %negate_multiply_fusion.6, f32[4,512,3072]{2,1,0:T(8,128)} %get-tuple-element.1122, s32[]{:T(128)} %get-tuple-element.1106), kind=kOutput, calls=%fused_computation.177.clone.1 | convolution fusion | flops 2533094400 | bytes 15742980 | tf_op jit(solution)/shard_map/while/body/eval_jaxpr/dot_general | solution.py:54
  599.5 19.1 %fusion.357 = f32[3072,768]{1,0:T(8,128)S(1)} fusion(f32[4,512,3072]{2,1,0:T(8,128)} %get-tuple-element.1122, s32[]{:T(128)} %get-tuple-element.1106, f32[4,512,768]{2,1,0:T(8,128)} %get-tuple-element.1125, f32[512]{0:T(512)S(1)} %negate_multiply_fusion.6, f32[512]{0:T(512)S(1)} %multiply_multiply_fusion.17, f32[512]{0:T(512)S(1)} %broadcast_multiply_fusion.10, ...), kind=kOutput, calls=%fused_computation.208.clone.1 | convolution fusion | flops 2521694208 | bytes 18100224 | tf_op jit(solution)/shard_map/while/body/eval_jaxpr/dot_general | solution.py:48
  618.7 19.2 %maximum_add_fusion.6 = f32[6144,768]{1,0:T(8,128)} fusion(f32[3072,768]{1,0:T(8,128)S(1)} %fusion.357, f32[3072,768]{1,0:T(8,128)S(1)} %fusion.359, f32[6144,768]{1,0:T(8,128)} %get-tuple-element.1107, pred[]{:T(512)S(6)} %compare.6), kind=kLoop, calls=%fused_computation.156.clone.1 | loop fusion | flops 14155776 | bytes 56623104 | tf_op jit(solution)/shard_map/while/body/eval_jaxpr/add | solution.py:308
  646.5 18.4 %convert_reduce_fusion.13 = (f32[3072]{0:T(1024)S(1)}, bf16[512,3072]{1,0:T(8,128)(2,1)S(1)}) fusion(bf16[6144,768]{1,0:T(8,128)(2,1)S(1)} %copy-done.20, f32[512,768]{1,0:T(8,128)S(1)} %get-tuple-element.993, f32[512]{0:T(512)S(1)} %negate_multiply_fusion.6, f32[4,512,3072]{2,1,0:T(8,128)} %get-tuple-element.1122, s32[]{:T(128)} %get-tuple-element.1106), kind=kOutput, calls=%fused_computation.177.clone.1 | convolution fusion | flops 2533094400 | bytes 15742980 | tf_op jit(solution)/shard_map/while/body/eval_jaxpr/dot_general | solution.py:54
  677.2 19.2 %fusion.357 = f32[3072,768]{1,0:T(8,128)S(1)} fusion(f32[4,512,3072]{2,1,0:T(8,128)} %get-tuple-element.1122, s32[]{:T(128)} %get-tuple-element.1106, f32[4,512,768]{2,1,0:T(8,128)} %get-tuple-element.1125, f32[512]{0:T(512)S(1)} %negate_multiply_fusion.6, f32[512]{0:T(512)S(1)} %multiply_multiply_fusion.17, f32[512]{0:T(512)S(1)} %broadcast_multiply_fusion.10, ...), kind=kOutput, calls=%fused_computation.208.clone.1 | convolution fusion | flops 2521694208 | bytes 18100224 | tf_op jit(solution)/shard_map/while/body/eval_jaxpr/dot_general | solution.py:48
  696.4 19.2 %maximum_add_fusion.6 = f32[6144,768]{1,0:T(8,128)} fusion(f32[3072,768]{1,0:T(8,128)S(1)} %fusion.357, f32[3072,768]{1,0:T(8,128)S(1)} %fusion.359, f32[6144,768]{1,0:T(8,128)} %get-tuple-element.1107, pred[]{:T(512)S(6)} %compare.6), kind=kLoop, calls=%fused_computation.156.clone.1 | loop fusion | flops 14155776 | bytes 56623104 | tf_op jit(solution)/shard_map/while/body/eval_jaxpr/add | solution.py:308
  724.2 18.4 %convert_reduce_fusion.13 = (f32[3072]{0:T(1024)S(1)}, bf16[512,3072]{1,0:T(8,128)(2,1)S(1)}) fusion(bf16[6144,768]{1,0:T(8,128)(2,1)S(1)} %copy-done.20, f32[512,768]{1,0:T(8,128)S(1)} %get-tuple-element.993, f32[512]{0:T(512)S(1)} %negate_multiply_fusion.6, f32[4,512,3072]{2,1,0:T(8,128)} %get-tuple-element.1122, s32[]{:T(128)} %get-tuple-element.1106), kind=kOutput, calls=%fused_computation.177.clone.1 | convolution fusion | flops 2533094400 | bytes 15742980 | tf_op jit(solution)/shard_map/while/body/eval_jaxpr/dot_general | solution.py:54
  754.9 19.1 %fusion.357 = f32[3072,768]{1,0:T(8,128)S(1)} fusion(f32[4,512,3072]{2,1,0:T(8,128)} %get-tuple-element.1122, s32[]{:T(128)} %get-tuple-element.1106, f32[4,512,768]{2,1,0:T(8,128)} %get-tuple-element.1125, f32[512]{0:T(512)S(1)} %negate_multiply_fusion.6, f32[512]{0:T(512)S(1)} %multiply_multiply_fusion.17, f32[512]{0:T(512)S(1)} %broadcast_multiply_fusion.10, ...), kind=kOutput, calls=%fused_computation.208.clone.1 | convolution fusion | flops 2521694208 | bytes 18100224 | tf_op jit(solution)/shard_map/while/body/eval_jaxpr/dot_general | solution.py:48
  774.1 19.2 %maximum_add_fusion.6 = f32[6144,768]{1,0:T(8,128)} fusion(f32[3072,768]{1,0:T(8,128)S(1)} %fusion.357, f32[3072,768]{1,0:T(8,128)S(1)} %fusion.359, f32[6144,768]{1,0:T(8,128)} %get-tuple-element.1107, pred[]{:T(512)S(6)} %compare.6), kind=kLoop, calls=%fused_computation.156.clone.1 | loop fusion | flops 14155776 | bytes 56623104 | tf_op jit(solution)/shard_map/while/body/eval_jaxpr/add | solution.py:308
  807.4 307.3 %while.62 = (s32[]{:T(128)}, f32[3072,768]{1,0:T(8,128)}, f32[4,768]{1,0:T(4,128)S(1)}, bf16[4,512,768]{2,1,0:T(8,128)(2,1)}, bf16[4,512,768]{2,1,0:T(8,128)(2,1...) while((s32[]{:T(128)}, f32[3072,768]{1,0:T(8,128)}, ...), condition=%wide.region_32.33_spmd.clone, body=%wide.region_25.32_spmd.clone.sunk | while | flops 7311070720 | bytes 260856176 | solution.py:329
  1115.6 39.4 %all-reduce = f32[13,768]{1,0:T(8,128)S(1)} all-reduce(f32[13,768]{1,0:T(8,128)S(1)} %pad_maximum_fusion.3), channel_id=4, replica_groups=mesh['wide'=8,'narrow'=4] {'wide','narrow'}, use_global_device_ids=true, to_apply=%region_35.36.clone | all-reduce | flops 9984 | bytes 79872
  1155.8 93.8 %reduce-scatter.4.cloned.1.call-done = f32[96,768]{1,0:T(8,128)} async-done(((f32[3072,768]{1,0:T(8,128)}), f32[96,768]{1,0:T(8,128)}) %reduce-scatter.4.cloned.1.call-update) | async-done | bytes 294928 | tf_op jit(solution)/shard_map/reduce_scatter | solution.py:334
  1251.7 210.0 %reduce-scatter.6.cloned.1.call-done = f32[192,768]{1,0:T(8,128)} async-done(((f32[6144,768]{1,0:T(8,128)}), f32[192,768]{1,0:T(8,128)}) %reduce-scatter.6.cloned.1.call-update) | async-done | bytes 589840 | tf_op jit(solution)/shard_map/reduce_scatter | solution.py:335
  (596 shorter events, 619.5 us)
Async XLA Ops:
  7.2 82.2 %all-gather.4.cloned.1.call-start = ((), (), s32[]{:S(2)}) async-start(), calls=%async_computation.2 | async-start | bytes 4866048 | tf_op jit(solution)/shard_map/all_gather | solution.py:273
  8.9 152.3 %all-gather.6.cloned.1.call-start = ((), (), s32[]{:S(2)}) async-start(), calls=%async_computation.3 | async-start | bytes 9732096 | tf_op jit(solution)/shard_map/all_gather | solution.py:276
  10.8 1238.8 %reduce-scatter.4.cloned.1.call-start = ((), (), s32[]{:S(2)}) async-start(), calls=%async_computation.4 | async-start | bytes 9732096 | tf_op jit(solution)/shard_map/reduce_scatter | solution.py:334
  468.5 338.3 %copy-start.14 = (f32[4,768]{1,0:T(4,128)S(1)}, f32[4,768]{1,0:T(4,128)}, u32[]{:S(2)}) copy-start(f32[4,768]{1,0:T(4,128)} %custom-call.3) | copy-start | bytes 36868
  489.9 27.0 %copy-start.6 = (f32[13,768]{1,0:T(8,128)}, f32[13,768]{1,0:T(8,128)S(1)}, u32[]{:S(2)}) copy-start(f32[13,768]{1,0:T(8,128)S(1)} %get-tuple-element.1124) | copy-start | bytes 119812 | tf_op jit(solution)/shard_map/while
  496.1 20.9 %slice-start.5 = ((s8[6291456]{0:T(1024)(128)(4,1)}), s8[4194304]{0:T(1024)(128)(4,1)S(1)}, s32[]{:S(2)}) async-start(s8[6291456]{0:T(1024)(128)(4,1)} %bitcast.361), calls=%async_computation.11 | async-start | bytes 8388608 | tf_op jit(solution)/shard_map/while
  560.2 27.0 %copy-start.6 = (f32[13,768]{1,0:T(8,128)}, f32[13,768]{1,0:T(8,128)S(1)}, u32[]{:S(2)}) copy-start(f32[13,768]{1,0:T(8,128)S(1)} %get-tuple-element.1124) | copy-start | bytes 119812 | tf_op jit(solution)/shard_map/while
  566.4 20.9 %slice-start.5 = ((s8[6291456]{0:T(1024)(128)(4,1)}), s8[4194304]{0:T(1024)(128)(4,1)S(1)}, s32[]{:S(2)}) async-start(s8[6291456]{0:T(1024)(128)(4,1)} %bitcast.361), calls=%async_computation.11 | async-start | bytes 8388608 | tf_op jit(solution)/shard_map/while
  618.7 19.2 %copy-start.7 = (f32[13,768]{1,0:T(8,128)S(1)}, f32[13,768]{1,0:T(8,128)}, u32[]{:S(2)}) copy-start(f32[13,768]{1,0:T(8,128)} %copy-done.6) | copy-start | bytes 119812 | tf_op jit(solution)/shard_map/while
  637.9 27.0 %copy-start.6 = (f32[13,768]{1,0:T(8,128)}, f32[13,768]{1,0:T(8,128)S(1)}, u32[]{:S(2)}) copy-start(f32[13,768]{1,0:T(8,128)S(1)} %get-tuple-element.1124) | copy-start | bytes 119812 | tf_op jit(solution)/shard_map/while
  644.1 20.9 %slice-start.5 = ((s8[6291456]{0:T(1024)(128)(4,1)}), s8[4194304]{0:T(1024)(128)(4,1)S(1)}, s32[]{:S(2)}) async-start(s8[6291456]{0:T(1024)(128)(4,1)} %bitcast.361), calls=%async_computation.11 | async-start | bytes 8388608 | tf_op jit(solution)/shard_map/while
  696.4 19.2 %copy-start.7 = (f32[13,768]{1,0:T(8,128)S(1)}, f32[13,768]{1,0:T(8,128)}, u32[]{:S(2)}) copy-start(f32[13,768]{1,0:T(8,128)} %copy-done.6) | copy-start | bytes 119812 | tf_op jit(solution)/shard_map/while
  715.6 27.0 %copy-start.6 = (f32[13,768]{1,0:T(8,128)}, f32[13,768]{1,0:T(8,128)S(1)}, u32[]{:S(2)}) copy-start(f32[13,768]{1,0:T(8,128)S(1)} %get-tuple-element.1124) | copy-start | bytes 119812 | tf_op jit(solution)/shard_map/while
  721.8 20.9 %slice-start.5 = ((s8[6291456]{0:T(1024)(128)(4,1)}), s8[4194304]{0:T(1024)(128)(4,1)S(1)}, s32[]{:S(2)}) async-start(s8[6291456]{0:T(1024)(128)(4,1)} %bitcast.361), calls=%async_computation.11 | async-start | bytes 8388608 | tf_op jit(solution)/shard_map/while
  1114.7 346.9 %reduce-scatter.6.cloned.1.call-start = ((), (), s32[]{:S(2)}) async-start(), calls=%async_computation.5 | async-start | bytes 19464192 | tf_op jit(solution)/shard_map/reduce_scatter | solution.py:335
  1114.8 40.3 %copy-start.17 = (f32[13,24]{1,0:T(8,128)S(1)}, f32[13,24]{1,0:T(8,128)}, u32[]{:S(2)}) copy-start(f32[13,24]{1,0:T(8,128)} %param.29) | copy-start | bytes 3748
  1114.8 40.3 %copy-start.18 = (f32[13,24]{1,0:T(8,128)S(1)}, f32[13,24]{1,0:T(8,128)}, u32[]{:S(2)}) copy-start(f32[13,24]{1,0:T(8,128)} %param.30) | copy-start | bytes 3748
  1114.8 40.3 %copy-start.19 = (f32[13,24]{1,0:T(8,128)S(1)}, f32[13,24]{1,0:T(8,128)}, u32[]{:S(2)}) copy-start(f32[13,24]{1,0:T(8,128)} %param.31) | copy-start | bytes 3748
  1114.8 134.8 %copy-start.11 = (f32[96,768]{1,0:T(8,128)S(1)}, f32[96,768]{1,0:T(8,128)}, u32[]{:S(2)}) copy-start(f32[96,768]{1,0:T(8,128)} %param.23) | copy-start | bytes 884740
  1114.8 134.8 %copy-start.15 = (f32[96,768]{1,0:T(8,128)S(1)}, f32[96,768]{1,0:T(8,128)}, u32[]{:S(2)}) copy-start(f32[96,768]{1,0:T(8,128)} %param.24) | copy-start | bytes 884740
  1114.8 134.8 %copy-start.16 = (f32[96,768]{1,0:T(8,128)S(1)}, f32[96,768]{1,0:T(8,128)}, u32[]{:S(2)}) copy-start(f32[96,768]{1,0:T(8,128)} %param.25) | copy-start | bytes 884740
  1114.9 346.8 %copy-start.5 = (f32[192,768]{1,0:T(8,128)S(1)}, f32[192,768]{1,0:T(8,128)}, u32[]{:S(2)}) copy-start(f32[192,768]{1,0:T(8,128)} %param.26) | copy-start | bytes 1769476
  1114.9 346.8 %copy-start.12 = (f32[192,768]{1,0:T(8,128)S(1)}, f32[192,768]{1,0:T(8,128)}, u32[]{:S(2)}) copy-start(f32[192,768]{1,0:T(8,128)} %param.27) | copy-start | bytes 1769476
  1114.9 346.8 %copy-start.13 = (f32[192,768]{1,0:T(8,128)S(1)}, f32[192,768]{1,0:T(8,128)}, u32[]{:S(2)}) copy-start(f32[192,768]{1,0:T(8,128)} %param.28) | copy-start | bytes 1769476
  (65 other events, 433.6 us)
Sparse Core Ops, SparseCore 0:
  11.4 66.4 all-gather.3
  81.2 79.9 all-gather.5
  1114.8 134.7 reduce-scatter.3
  1255.9 205.7 reduce-scatter.5
where the time goes:
time: 1480 us; the launch traced here: 1470 us
  matrix products  541 us (37%)
  waiting for transfers between devices  376 us (25%)
  other arithmetic  225 us (15%)
  local copies, waits for them, and re-layouts  146 us (10%)
  blocking collectives  111 us (8%)
  loops' own time  57.7 us (4%)
    reduce_scatter x1, waiting for transfers between devices, local(): lax.psum_scatter(feedforward_grad, ('wide', 'narrow'), scatter_dimension=...  210 us
    dot_general x12, matrix products, contract_cols(): lax.dot_general(left, right, (((1,), (1,)), ((), ())), preferred_element_...  115 us
    dot_general x12, matrix products, contract_rows(): lax.dot_general(left, right, (((0,), (0,)), ((), ())), preferred_element_...  107 us
    reduce_scatter x1, waiting for transfers between devices, local(): lax.psum_scatter(attention_grad, ('wide', 'narrow'), scatter_dimension=0,...  93.8 us
    dot_general x4, matrix products, forward_sequence(): jnp.dot(activated, feedforward_all[FF:], preferred_element_type=jnp.float32)  73.1 us
    all_gather x1, waiting for transfers between devices, local(): lax.all_gather(feedforward_master.astype(jnp.bfloat16), ('wide', 'narrow'...  71.8 us
    all_gather x1, blocking collectives, local(): lax.all_gather(vector_master.astype(jnp.bfloat16), ('wide', 'narrow'), ax...  71.6 us
    add x8, other arithmetic, feedforward_turn(): return ((running[0] + weight_part, running[1] + vector_part), first_grad)  69.7 us
  transfers between devices with their start and end apart: 4, of which 3 were waited for; matrix products, arithmetic and copies ran while one was open for 1% of the time, Pallas kernels for 0%

commit v1 on v0

v1 whole, which is shorter than its diff:
```python
from functools import partial
import jax, jax.numpy as jnp
from jax import lax
from jax.experimental import pallas as pl
from jax.experimental.pallas import tpu as pltpu
from jax.sharding import PartitionSpec as P

D = 768
FF = 3072
HEADS = 12
HEAD_DIM = 64
NORM_EPS = 1e-05
AWAY = -1e30
F32, BF16 = jnp.float32, jnp.bfloat16
ERFC = (0.11841221385764535, 0.11979147087435008, 0.09737185909338779, 0.13434283549706147,
        -0.0652102059595758, 0.2202795624136942, -0.16009561537425632, 0.035107795064101)
VMEM = pltpu.VMEM


def nn(a, b):
    return lax.dot_general(a, b, (((1,), (0,)), ((), ())), preferred_element_type=F32)

def nt(a, b):
    return lax.dot_general(a, b, (((1,), (1,)), ((), ())), preferred_element_type=F32)

def tn(a, b):
    return lax.dot_general(a, b, (((0,), (0,)), ((), ())), preferred_element_type=F32)

def whole(shape):
    return pl.BlockSpec(shape, lambda i: (0,) * len(shape), pipeline_mode=pl.Buffered(1))

def gelu_pair(h):
    size = jnp.abs(h)
    t = 1.0 / (1.0 + (0.42 * 0.7071067811865476) * size)
    bell = jnp.exp(h * h * -0.5)
    poly = jnp.full_like(t, ERFC[-1])
    for coef in ERFC[-2::-1]:
        poly = poly * t + coef
    tail = poly * t * bell
    below = jnp.where(h < 0, tail, 1.0 - tail)
    return h * below, below + h * bell * 0.3989422804014327

def column_of(row):
    return jnp.transpose(jnp.broadcast_to(row, (8, row.shape[1])))[:, :1]

def group_of(seg, feat):
    both = seg * 16 + feat
    return column_of(both) == both

def k1_body(tok_ref, seg_ref, feat_ref, w_ref, vec_ref, mixed_ref, q_ref, k_ref, v_ref, ctx_ref, lse_ref, bias_scr):
    i = pl.program_id(0)
    seg = seg_ref[pl.ds(i, 1), :]
    feat = feat_ref[pl.ds(i, 1), :]
    length = seg.shape[1]
    bias_scr[...] = jnp.where(column_of(seg) == seg, 0.0, AWAY)
    group = group_of(seg, feat)
    members = jnp.sum(group.astype(F32), axis=1, keepdims=True)
    tok = tok_ref[...]
    merging = nn(group.astype(F32).astype(BF16), tok) / members
    mixed = tok.astype(F32) + vec_ref[0:1, :] * merging
    mixed_ref[...] = mixed
    mb = mixed.astype(BF16)
    q_ref[...] = ((nn(mb, w_ref[0:D, :]) + vec_ref[1:2, :]) * 0.125).astype(BF16)
    k_ref[...] = nn(mb, w_ref[D:2 * D, :]).astype(BF16)
    v_ref[...] = (nn(mb, w_ref[2 * D:3 * D, :]) + vec_ref[2:3, :]).astype(BF16)
    lane = lax.broadcasted_iota(jnp.int32, (length, 128), 1)
    low = lane < HEAD_DIM
    lse_ref[...] = jnp.zeros_like(lse_ref)

    def pair(p, carry):
        at = pl.ds(pl.multiple_of(p * 128, 128), 128)
        qp = q_ref[:, at]
        kp = k_ref[:, at]
        vp = v_ref[:, at]
        outs = []
        zero = jnp.zeros_like(qp)
        for half in range(2):
            mine = low if half == 0 else jnp.logical_not(low)
            s = nt(jnp.where(mine, qp, zero), kp) + bias_scr[...]
            top = jnp.max(s, axis=1, keepdims=True)
            e = jnp.exp(s - top)
            total = jnp.sum(e, axis=1, keepdims=True)
            o = nn(e.astype(BF16), vp) * (1.0 / total)
            outs.append(o)
            lse_ref[...] = jnp.where(lane == 2 * p + half, top + jnp.log(total), lse_ref[...])
        ctx_ref[:, at] = jnp.where(low, outs[0], outs[1]).astype(BF16)
        return carry
    lax.fori_loop(0, HEADS // 2, pair, 0)


def k1(tokens, seg, feat, att, vec):
    seqs, length = seg.shape
    blk = pl.BlockSpec((length, D), lambda i: (i, 0))
    n = seqs * length
    o = lambda dt: jax.ShapeDtypeStruct((n, D), dt)
    return pl.pallas_call(
        k1_body, grid=(seqs,),
        in_specs=[blk, whole((seqs, length)), whole((seqs, length)), pl.BlockSpec((3 * D, D), lambda i: (0, 0), pipeline_mode=pl.Buffered(1)), whole(vec.shape)],
        out_specs=[blk] * 5 + [pl.BlockSpec((length, 128), lambda i: (i, 0))],
        out_shape=[o(F32), o(BF16), o(BF16), o(BF16), o(BF16), jax.ShapeDtypeStruct((n, 128), F32)],
        scratch_shapes=[VMEM((length, length), F32)],
        name="mix_attend",
    )(tokens, seg, feat, att, vec)

def norm_parts(z):
    mean = jnp.mean(z, axis=1, keepdims=True)
    c = z - mean
    var = jnp.mean(c * c, axis=1, keepdims=True)
    inv = lax.rsqrt(var + NORM_EPS)
    return c * inv, inv

def norm_pull(g, xhat, inv):
    a = jnp.mean(g, axis=1, keepdims=True)
    b = jnp.mean(g * xhat, axis=1, keepdims=True)
    return (g - a - xhat * b) * inv

def colsum(x):
    return jnp.sum(x, axis=0, keepdims=True)

def k2_body(mixed_ref, ctx_ref, cot_ref, wo_ref, wf_ref, vec_ref,
            out_ref, first_ref, fb_ref, dctx_ref, act_ref, hg_ref, nb_ref, bg_ref, vg_ref, gp_scr, sum_scr):
    @pl.when(pl.program_id(0) == 0)
    def _():
        vg_ref[...] = jnp.zeros_like(vg_ref)
    ex = FF // D
    first_sum = mixed_ref[...] + nn(ctx_ref[...], wo_ref[...]) + vec_ref[3:4, :]
    xhat1, inv1 = norm_parts(first_sum)
    normed = xhat1 * vec_ref[4:5, :] + vec_ref[5:6, :]
    nb_ref[...] = normed.astype(BF16)
    sum_scr[...] = normed + vec_ref[6 + ex:7 + ex, :]
    for c in range(ex):
        at = pl.ds(c * D, D)
        h = nt(nb_ref[...], wf_ref[at, :]) + vec_ref[6 + c:7 + c, :]
        act, slope = gelu_pair(h)
        act_ref[:, at] = act.astype(BF16)
        gp_scr[:, at] = slope.astype(gp_scr.dtype)
        sum_scr[...] += nn(act_ref[:, at], wf_ref[pl.ds(FF + c * D, D), :])
    xhat2, inv2 = norm_parts(sum_scr[...])
    out_ref[...] = (xhat2 * vec_ref[7 + ex:8 + ex, :] + vec_ref[8 + ex:9 + ex, :]).astype(BF16)
    cot = cot_ref[...].astype(F32)
    vg_ref[4 + ex:5 + ex, :] += colsum(cot * xhat2)
    vg_ref[5 + ex:6 + ex, :] += colsum(cot)
    gs = norm_pull(cot * vec_ref[7 + ex:8 + ex, :], xhat2, inv2)
    vg_ref[3 + ex:4 + ex, :] += colsum(gs)
    bg_ref[...] = gs.astype(BF16)
    sum_scr[...] = gs
    for c in range(ex):
        at = pl.ds(c * D, D)
        hg = nt(bg_ref[...], wf_ref[pl.ds(FF + c * D, D), :]) * gp_scr[:, at].astype(F32)
        vg_ref[3 + c:4 + c, :] += colsum(hg)
        hg_ref[:, at] = hg.astype(BF16)
        sum_scr[...] += nn(hg_ref[:, at], wf_ref[at, :])
    ng = sum_scr[...]
    vg_ref[1:2, :] += colsum(ng * xhat1)
    vg_ref[2:3, :] += colsum(ng)
    fgr = norm_pull(ng * vec_ref[4:5, :], xhat1, inv1)
    vg_ref[0:1, :] += colsum(fgr)
    first_ref[...] = fgr
    fb_ref[...] = fgr.astype(BF16)
    dctx_ref[...] = nt(fb_ref[...], wo_ref[...]).astype(BF16)


def k2(mixed, ctx, cot, att, ff, vec, tile=256):
    n = mixed.shape[0]
    blk = pl.BlockSpec((tile, D), lambda i: (i, 0))
    wide = pl.BlockSpec((tile, FF), lambda i: (i, 0))
    o = lambda w, dt: jax.ShapeDtypeStruct((n, w), dt)
    return pl.pallas_call(
        k2_body, grid=(n // tile,),
        in_specs=[blk, blk, blk, pl.BlockSpec((D, D), lambda i: (3, 0), pipeline_mode=pl.Buffered(1)), whole(ff.shape), whole(vec.shape)],
        out_specs=[blk, blk, blk, blk, wide, wide, blk, blk, pl.BlockSpec((16, D), lambda i: (0, 0))],
        out_shape=[o(D, BF16), o(D, F32), o(D, BF16), o(D, BF16), o(FF, BF16), o(FF, BF16), o(D, BF16), o(D, BF16), jax.ShapeDtypeStruct((16, D), F32)],
        scratch_shapes=[VMEM((tile, FF), F32), VMEM((tile, D), F32)],
        name="feed_forward",
    )(mixed, ctx, cot, att, ff, vec)

def k3_body(q_ref, k_ref, v_ref, ctx_ref, dctx_ref, lse_ref, seg_ref, dq_ref, dk_ref, dv_ref, vg_ref, bias_scr, lse_scr, del_scr):
    i = pl.program_id(0)
    @pl.when(i == 0)
    def _():
        vg_ref[...] = jnp.zeros_like(vg_ref)
    seg = seg_ref[pl.ds(i, 1), :]
    length = seg.shape[1]
    bias_scr[...] = jnp.where(column_of(seg) == seg, 0.0, AWAY)
    lse_scr[...] = jnp.transpose(lse_ref[...])[:16, :]
    prod = dctx_ref[...].astype(F32) * ctx_ref[...].astype(F32)
    pick = (lax.broadcasted_iota(jnp.int32, (16, D), 1) // HEAD_DIM == lax.broadcasted_iota(jnp.int32, (16, D), 0)).astype(F32)
    del_scr[...] = lax.dot_general(pick, prod, (((1,), (1,)), ((), ())), precision=lax.Precision.HIGHEST, preferred_element_type=F32)
    low = lax.broadcasted_iota(jnp.int32, (length, 128), 1) < HEAD_DIM

    def pair(p, carry):
        at = pl.ds(pl.multiple_of(p * 128, 128), 128)
        qp, kp, vp, op = q_ref[:, at], k_ref[:, at], v_ref[:, at], dctx_ref[:, at]
        zero = jnp.zeros_like(qp)
        got = []
        for half in range(2):
            mine = low if half == 0 else jnp.logical_not(low)
            st = nt(jnp.where(mine, kp, zero), qp) + bias_scr[...]
            pt = jnp.exp(st - lse_scr[pl.ds(2 * p + half, 1), :])
            dv = nn(pt.astype(BF16), op)
            dpt = nt(jnp.where(mine, vp, zero), op)
            dst = (pt * (dpt - del_scr[pl.ds(2 * p + half, 1), :])).astype(BF16)
            dk = nn(dst, qp)
            dq = tn(dst, kp)
            got.append((dq, dk, dv))
        dq, dk, dv = (jnp.where(low, a, b) for a, b in zip(*got))
        dqb = dq.astype(BF16) * jnp.bfloat16(0.125)
        dvb = dv.astype(BF16)
        dq_ref[:, at] = dqb
        dk_ref[:, at] = dk.astype(BF16)
        dv_ref[:, at] = dvb
        vg_ref[0:1, at] += colsum(dqb.astype(F32))
        vg_ref[1:2, at] += colsum(dvb.astype(F32))
        return carry
    lax.fori_loop(0, HEADS // 2, pair, 0)


def k3(q, k, v, ctx, dctx, lse, seg):
    seqs, length = seg.shape
    n = seqs * length
    blk = pl.BlockSpec((length, D), lambda i: (i, 0))
    o = jax.ShapeDtypeStruct((n, D), BF16)
    return pl.pallas_call(
        k3_body, grid=(seqs,),
        in_specs=[blk] * 5 + [pl.BlockSpec((length, 128), lambda i: (i, 0)), whole((seqs, length))],
        out_specs=[blk] * 3 + [pl.BlockSpec((8, D), lambda i: (0, 0))],
        out_shape=[o, o, o, jax.ShapeDtypeStruct((8, D), F32)],
        scratch_shapes=[VMEM((length, length), F32), VMEM((16, length), F32), VMEM((16, length), F32)],
        name="attend_back",
    )(q, k, v, ctx, dctx, lse, seg)

def k4_body(first_ref, dq_ref, dk_ref, dv_ref, tok_ref, mixed_ref, seg_ref, feat_ref, w_ref, vec_ref, tg_ref, vg_ref):
    i = pl.program_id(0)
    @pl.when(i == 0)
    def _():
        vg_ref[...] = jnp.zeros_like(vg_ref)
    group = group_of(seg_ref[pl.ds(i, 1), :], feat_ref[pl.ds(i, 1), :])
    gf = group.astype(F32)
    members = jnp.sum(gf, axis=1, keepdims=True)
    gb = gf.astype(BF16)
    tok = tok_ref[...]
    merging = nn(gb, tok) / members
    mg = (first_ref[...] + nt(dq_ref[...], w_ref[0:D, :]) + nt(dk_ref[...], w_ref[D:2 * D, :])
          + nt(dv_ref[...], w_ref[2 * D:3 * D, :]))
    vg_ref[0:1, :] += colsum(mg * merging)
    spread = (vec_ref[0:1, :] * mg / members).astype(BF16)
    tg_ref[...] = (mg + nn(gb, spread)).astype(BF16)


def k4(first, dq, dk, dv, tokens, mixed, seg, feat, att, vec):
    seqs, length = seg.shape
    n = seqs * length
    blk = pl.BlockSpec((length, D), lambda i: (i, 0))
    return pl.pallas_call(
        k4_body, grid=(seqs,),
        in_specs=[blk] * 5 + [blk, whole((seqs, length)), whole((seqs, length)), pl.BlockSpec((3 * D, D), lambda i: (0, 0), pipeline_mode=pl.Buffered(1)), whole(vec.shape)],
        out_specs=[blk, pl.BlockSpec((8, D), lambda i: (0, 0))],
        out_shape=[jax.ShapeDtypeStruct((n, D), BF16), jax.ShapeDtypeStruct((8, D), F32)],
        name="token_grad",
    )(first, dq, dk, dv, tokens, mixed, seg, feat, att, vec)

def adam_step(master, first, second, gradient, rate):
    first_new = BETA * first + (1.0 - BETA) * gradient
    second_new = BETA * second + (1.0 - BETA) * gradient * gradient
    correction = 1.0 - BETA**ADAM_STEP
    master_new = master - rate * (
        first_new / correction / (jnp.sqrt(second_new / correction) + ADAM_EPS) + DECAY * master
    )
    return (master_new, first_new, second_new)


BETA = 0.5
ADAM_STEP = 3
ADAM_EPS = 1e-08
DECAY = 0.01
VECTOR_RATE = 0.1
BOTH = ("wide", "narrow")


def rates(rows, split, first_rate, second_rate):
    index = (lax.axis_index(BOTH) * rows + jnp.arange(rows))[:, None]
    return jnp.where(index < split, first_rate, second_rate)


def local(tokens, cotangent, segment_ids, feature_ids,
          attention_master, attention_first, attention_second,
          feedforward_master, feedforward_first, feedforward_second,
          vector_master, vector_first, vector_second):
    gather = partial(lax.all_gather, axis_name=BOTH, tiled=True)
    att = gather(attention_master.astype(BF16), axis=0)
    ff = gather(feedforward_master.astype(BF16), axis=0)
    vec = jnp.pad(gather(vector_master.astype(BF16), axis=1).astype(F32), ((0, 3), (0, 0)))
    seg, feat = segment_ids, feature_ids
    mixed, q, k, v, ctx, lse = k1(tokens, seg, feat, att, vec)
    out, first, fb, dctx, act, hg, nb, bg, vg2 = k2(mixed, ctx, cotangent, att, ff, vec)
    scatter = partial(lax.psum_scatter, axis_name=BOTH, tiled=True)
    ff_grad = jnp.concatenate([tn(hg, nb), tn(act, bg)], axis=0).astype(BF16)
    ff_owned = scatter(ff_grad, scatter_dimension=0).astype(F32)
    dq, dk, dv, vg3 = k3(q, k, v, ctx, dctx, lse, seg)
    mb = mixed.astype(BF16)
    att_grad = jnp.concatenate([tn(mb, dq), tn(mb, dk), tn(mb, dv), tn(ctx, fb)], axis=0).astype(BF16)
    att_owned = scatter(att_grad, scatter_dimension=0).astype(F32)
    token_grads, vg4 = k4(first, dq, dk, dv, tokens, mixed, seg, feat, att, vec)
    vec_grad = jnp.concatenate([vg4[0:1], vg3[0:2], vg2[:10]], axis=0)
    vec_owned = scatter(vec_grad, scatter_dimension=1)
    ff_rate = rates(feedforward_master.shape[0], FF, D ** (-0.5), FF ** (-0.5))
    att_rate = rates(attention_master.shape[0], 3 * D, D ** (-0.5), (D // 64) ** (-0.5))
    f_new = adam_step(feedforward_master, feedforward_first, feedforward_second, ff_owned, ff_rate)
    a_new = adam_step(attention_master, attention_first, attention_second, att_owned, att_rate)
    v_new = adam_step(vector_master, vector_first, vector_second, vec_owned, VECTOR_RATE)
    result = [out, token_grads]
    for new in (a_new, f_new, v_new):
        result += [*new, new[0].astype(BF16)]
    return tuple(result)


def solution(mesh):
    rows, cols = P(BOTH, None), P(None, BOTH)
    return jax.shard_map(
        local, mesh=mesh,
        in_specs=(rows,) * 10 + (cols,) * 3,
        out_specs=(rows,) * 10 + (cols,) * 4,
        check_vma=False,
    )
```

time: 1480 us -> 578 us (0.39)
  matrix products: 541 us -> 41.3 us
  waiting for transfers between devices: 376 us -> 173 us
  other arithmetic: 225 us -> 28.2 us
  Pallas kernels: 0 us -> 196 us
  local copies, waits for them, and re-layouts: 146 us -> 3.73 us
  loops' own time: 57.7 us -> 0 us
    dot_general x84 -> x6, matrix products: 541 us -> 41.3 us  [tn(): lax.dot_general(a, b, (((0,), (0,)), ((), ())), preferred_element_type=F32)]
    pallas_call x0 -> x4, Pallas kernels: none -> 196 us  [the longest x1 84.1 us: k2(): pl.pallas_call(k2_body, grid=(n // tile,), in_specs=[blk, blk, blk, pl.Bl...]
    reduce_scatter x2, waiting for transfers between devices: 304 us -> 139 us  [the longest x1 139 us: local(): ff_owned = scatter(ff_grad, scatter_dimension=0).astype(F32)]
    add x16 -> x0, other arithmetic: 102 us -> none  [the longest x8 69.7 us: feedforward_turn(): return ((running[0] + weight_part, running[1] + vector_part), first_grad)]
    reduce_sum x60 -> x0, other arithmetic: 68.1 us -> none  [the longest x8 19.2 us: layer_norm(): return centred * lax.rsqrt(variance + NORM_EPS) * gain_row + shift_row]
    another operation x3 -> x0, loops' own time: 57.7 us -> none  [the longest x1 35.7 us: local(): lax.scan(feedforward_turn, start_late, (stored, grad_blocks))]
    dynamic_slice x36 -> x0, local copies, waits for them, and re-layouts: 38.8 us -> none  [the longest x28 23.6 us: local(): lax.map(run_forward, (token_blocks, segment_ids, feature_ids))]
    all_gather x2, waiting for transfers between devices: 71.8 us -> 34.7 us  [the longest x1 34.7 us: local(): ff = gather(feedforward_master.astype(BF16), axis=0)]
  transfers between devices with their start and end apart: 4 -> 4, of which waited for: 3 -> 2; matrix products, arithmetic and copies ran while one was open for 1% -> 9% of each run, Pallas kernels for 0% -> 11%
where the time goes in v1:
time: 578 us; the launch traced here: 568 us
  Pallas kernels  196 us (34%)
  waiting for transfers between devices  173 us (30%)
  blocking collectives  111 us (19%)
  matrix products  41.3 us (7%)
  other arithmetic  28.2 us (5%)
  between operations  14.3 us (2%)
    reduce_scatter x1, waiting for transfers between devices, local(): ff_owned = scatter(ff_grad, scatter_dimension=0).astype(F32)  139 us
    pallas_call x1, Pallas kernels, k2(): pl.pallas_call(k2_body, grid=(n // tile,), in_specs=[blk, blk, blk, pl.Bl...  84.1 us
    all_gather x1, blocking collectives, local(): gather(vector_master.astype(BF16), axis=1).astype(F32)  71.7 us
    pallas_call x1, Pallas kernels, k3(): pl.pallas_call(k3_body, grid=(seqs,), in_specs=[blk] * 5 + [pl.BlockSpec(...  49 us
    pallas_call x1, Pallas kernels, k1(): pl.pallas_call(k1_body, grid=(seqs,), in_specs=[blk, whole((seqs, length)...  42.5 us
    dot_general x6, matrix products, tn(): lax.dot_general(a, b, (((0,), (0,)), ((), ())), preferred_element_type=F32)  41.3 us
    unnamed x1, blocking collectives  39.7 us
    all_gather x1, waiting for transfers between devices, local(): ff = gather(feedforward_master.astype(BF16), axis=0)  34.7 us
  transfers between devices with their start and end apart: 4, of which 2 were waited for; matrix products, arithmetic and copies ran while one was open for 9% of the time, Pallas kernels for 11%

profile of v1, /device:TPU:0, one launch (start us, length us, event | category | flops | bytes accessed | tf_op | source)
XLA Modules:
  0.0 568.4 jit_solution(11861665429638621605)
XLA Ops:
  7.2 1.6 convert_element_type.32
  8.9 1.8 convert_element_type.34
  11.5 71.7 %all-gather = bf16[32,24,13]{1,2,0:T(8,128)(2,1)S(1)} all-gather(bf16[1,24,13]{1,2,0:T(8,128)(2,1)S(1)} %convert_bitcast_fusion), channel_id=1, replica_groups=mesh['wide'=8,'narrow'=4] {'wide','narrow'}, dimensions={0}, use_global_device_ids=true | all-gather | bytes 20592 | tf_op jit(solution)/shard_map/all_gather | solution.py:292
  84.0 42.5 %mix_attend.1 = (f32[2048,768]{1,0:T(8,128)}, bf16[2048,768]{1,0:T(8,128)(2,1)}, bf16[2048,768]{1,0:T(8,128)(2,1)}, bf16[2048,768]{1,0:T(8,128)(2,1)}, bf16[2048,768]{1,0:T(8,128)(2,1)}, /*index=5*/f32[2048,128]{1,0:T(8,128)}) custom-call(bf16[2048,768]{1,0:T(8,128)(2,1)} %tok_ref.3, s32[4,512]{1,0:T(4,128)} %seg_ref.5, s32[4,512]{1,0:T(4,128)} %feat_ref.3, ...), custom_call_target="tpu_custom_call" | custom-call | tf_op jit(solution)/shard_map/mix_attend/pallas_call | solution.py:96
  126.5 34.7 %all-gather.6.cloned.1.call-done.wf_ref = bf16[6144,768]{1,0:T(8,128)(2,1)} async-done(((bf16[192,768]{1,0:T(8,128)(2,1)}), bf16[6144,768]{1,0:T(8,128)(2,1)}) %all-gather.6.cloned.1.call-update) | async-done | bytes 9437200 | tf_op jit(solution)/shard_map/all_gather | solution.py:291
  161.3 84.1 %feed_forward.1 = (bf16[2048,768]{1,0:T(8,128)(2,1)}, f32[2048,768]{1,0:T(8,128)}, bf16[2048,768]{1,0:T(8,128)(2,1)}, bf16[2048,768]{1,0:T(8,128)(2,1)}, bf16[20...) custom-call(f32[2048,768]{1,0:T(8,128)} %get-tuple-element.35.mixed_, ...), custom_call_target="tpu_custom_call" | custom-call | tf_op jit(solution)/shard_map/feed_forward/pallas_call | solution.py:168
  245.4 49.0 %attend_back.1 = (bf16[2048,768]{1,0:T(8,128)(2,1)}, bf16[2048,768]{1,0:T(8,128)(2,1)}, bf16[2048,768]{1,0:T(8,128)(2,1)}, f32[8,768]{1,0:T(8,128)}) custom-call(bf16[2048,768]{1,0:T(8,128)(2,1)} %get-tuple-element.39.q_ref, bf16[2048,768]{1,0:T(8,128)(2,1)} %get-tuple-element.40.k_ref, bf16[2048,768]{1,0:T(8,128)(2,1)} %get-tuple-element.41.v_ref, ...), custom_call_target="tpu_custom_call" | custom-call | tf_op jit(solution)/shard_map/attend_back/pallas_call | solution.py:223
  294.4 6.5 %convolution_convert_fusion.5 = bf16[768,768]{1,0:T(8,128)(2,1)S(1)} fusion(bf16[2048,768]{1,0:T(8,128)(2,1)} %get-tuple-element.44.dq_ref, f32[2048,768]{1,0:T(8,128)} %get-tuple-element.35.mixed_ref), kind=kOutput, calls=%fused_computation.7 | convolution fusion | flops 2418081792 | bytes 10616832 | tf_op jit(solution)/shard_map/dot_general | solution.py:27
  301.0 2.7 convolution_convert_fusion.4
  303.7 2.7 convolution_convert_fusion.3
  306.5 2.7 convolution_convert_fusion.2
  309.2 2.5 pad_maximum_fusion.1
  311.8 1.8 copy-done.15
  313.6 13.5 %convolution_convert_fusion.1 = bf16[3072,768]{1,0:T(8,128)(2,1)S(1)} fusion(bf16[2048,3072]{1,0:T(8,128)(2,1)} %get-tuple-element.49, bf16[2048,768]{1,0:T(8,128)(2,1)S(1)} %copy-done.15), kind=kOutput, calls=%fused_computation.2 | convolution fusion | flops 9666035712 | bytes 20447232 | tf_op jit(solution)/shard_map/dot_general | solution.py:27
  327.1 13.3 %convolution_convert_fusion = bf16[3072,768]{1,0:T(8,128)(2,1)S(1)} fusion(bf16[2048,3072]{1,0:T(8,128)(2,1)} %get-tuple-element.51, bf16[2048,768]{1,0:T(8,128)(2,1)S(1)} %copy-done.14), kind=kOutput, calls=%fused_computation.1 | convolution fusion | flops 9666035712 | bytes 20447232 | tf_op jit(solution)/shard_map/dot_general | solution.py:27
  340.4 15.7 %pad_maximum_fusion = bf16[6144,768]{1,0:T(8,128)(2,1)} fusion(bf16[3072,768]{1,0:T(8,128)(2,1)S(1)} %convolution_convert_fusion, bf16[3072,768]{1,0:T(8,128)(2,1)S(1)} %convolution_convert_fusion.1), kind=kLoop, calls=%fused_computation | loop fusion | flops 18874368 | bytes 18874368 | tf_op jit(solution)/shard_map/concatenate | solution.py:297
  356.2 20.4 %token_grad.1 = (bf16[2048,768]{1,0:T(8,128)(2,1)}, f32[8,768]{1,0:T(8,128)}) custom-call(f32[2048,768]{1,0:T(8,128)} %get-tuple-element.38.first_ref, bf16[2048,768]{1,0:T(8,128)(2,1)} %get-tuple-element.44.dq_ref, bf16[2048,768]{1,0:T(8,128)(2,1)} %get-tuple-element.45.dk_ref, bf16[2048,768]{1,0:T(8,128)(2,1)} %get-tuple-element.46.dv_ref, ...), custom_call_target="tpu_custom_call" | custom-call | tf_op jit(solution)/shard_map/token_grad/pallas_call | solution.py:254
  376.6 0.7 slice.9
  377.3 0.7 slice.10
  378.1 39.7 %all-reduce.1 = f32[13,768]{1,0:T(8,128)S(1)} all-reduce(f32[13,768]{1,0:T(8,128)S(1)} %pad_maximum_fusion.2), channel_id=4, replica_groups=mesh['wide'=8,'narrow'=4] {'wide','narrow'}, use_global_device_ids=true, to_apply=%region_2.3.clone | all-reduce | flops 9984 | bytes 79872
  417.8 0.7 fusion.6
  418.5 2.0 fusion.10
  420.6 138.5 %reduce-scatter.6.cloned.1.call-done = bf16[192,768]{1,0:T(8,128)(2,1)} async-done(((bf16[6144,768]{1,0:T(8,128)(2,1)}), bf16[192,768]{1,0:T(8,128)(2,1)}) %reduce-scatter.6.cloned.1.call-update) | async-done | bytes 294928 | tf_op jit(solution)/shard_map/reduce_scatter | solution.py:298
  559.1 2.6 fusion.8
  (50 shorter events, 2.0 us)
Async XLA Ops:
  7.2 76.8 %all-gather.4.cloned.1.call-start = ((), (), s32[]{:S(2)}) async-start(), calls=%async_computation.2 | async-start | bytes 4866048 | tf_op jit(solution)/shard_map/all_gather | solution.py:290
  8.9 152.4 %all-gather.6.cloned.1.call-start = ((), (), s32[]{:S(2)}) async-start(), calls=%async_computation.3 | async-start | bytes 9732096 | tf_op jit(solution)/shard_map/all_gather | solution.py:291
  10.8 407.8 %reduce-scatter.4.cloned.1.call-start = ((), (), s32[]{:S(2)}) async-start(), calls=%async_computation.4 | async-start | bytes 4866048 | tf_op jit(solution)/shard_map/reduce_scatter | solution.py:302
  294.4 6.5 %copy-start = (f32[2048,768]{1,0:T(8,128)S(1)}, f32[2048,768]{1,0:T(8,128)}, u32[]{:S(2)}) copy-start(f32[2048,768]{1,0:T(8,128)} %get-tuple-element.35.mixed_ref) | copy-start | bytes 18874372
  294.4 6.6 %copy-start.2 = (bf16[2048,768]{1,0:T(8,128)(2,1)S(1)}, bf16[2048,768]{1,0:T(8,128)(2,1)}, u32[]{:S(2)}) copy-start(bf16[2048,768]{1,0:T(8,128)(2,1)} %get-tuple-element.45.dk_ref) | copy-start | bytes 9437188
  301.0 2.7 copy-start.3
  303.7 2.7 copy-start.1
  303.7 2.8 copy-start.16
  311.7 1.9 copy-start.15
  311.7 247.3 %reduce-scatter.6.cloned.1.call-start = ((), (), s32[]{:S(2)}) async-start(), calls=%async_computation.5 | async-start | bytes 9732096 | tf_op jit(solution)/shard_map/reduce_scatter | solution.py:298
  313.6 13.5 %copy-start.14 = (bf16[2048,768]{1,0:T(8,128)(2,1)S(1)}, bf16[2048,768]{1,0:T(8,128)(2,1)}, u32[]{:S(2)}) copy-start(bf16[2048,768]{1,0:T(8,128)(2,1)} %get-tuple-element.52) | copy-start | bytes 9437188
  356.1 22.0 %copy-start.10 = (f32[16,768]{1,0:T(8,128)S(1)}, f32[16,768]{1,0:T(8,128)}, u32[]{:S(2)}) copy-start(f32[16,768]{1,0:T(8,128)} %get-tuple-element.55) | copy-start | bytes 147460
  356.1 61.7 %copy-start.11 = (f32[13,24]{1,0:T(8,128)S(1)}, f32[13,24]{1,0:T(8,128)}, u32[]{:S(2)}) copy-start(f32[13,24]{1,0:T(8,128)} %param.23) | copy-start | bytes 3748
  356.1 61.7 %copy-start.12 = (f32[13,24]{1,0:T(8,128)S(1)}, f32[13,24]{1,0:T(8,128)}, u32[]{:S(2)}) copy-start(f32[13,24]{1,0:T(8,128)} %param.24) | copy-start | bytes 3748
  356.1 61.7 %copy-start.13 = (f32[13,24]{1,0:T(8,128)S(1)}, f32[13,24]{1,0:T(8,128)}, u32[]{:S(2)}) copy-start(f32[13,24]{1,0:T(8,128)} %param.25) | copy-start | bytes 3748
  356.2 62.4 %copy-start.5 = (f32[96,768]{1,0:T(8,128)S(1)}, f32[96,768]{1,0:T(8,128)}, u32[]{:S(2)}) copy-start(f32[96,768]{1,0:T(8,128)} %param.17) | copy-start | bytes 884740
  356.2 62.4 %copy-start.8 = (f32[96,768]{1,0:T(8,128)S(1)}, f32[96,768]{1,0:T(8,128)}, u32[]{:S(2)}) copy-start(f32[96,768]{1,0:T(8,128)} %param.18) | copy-start | bytes 884740
  356.2 62.4 %copy-start.9 = (f32[96,768]{1,0:T(8,128)S(1)}, f32[96,768]{1,0:T(8,128)}, u32[]{:S(2)}) copy-start(f32[96,768]{1,0:T(8,128)} %param.19) | copy-start | bytes 884740
  356.2 202.9 %copy-start.4 = (f32[192,768]{1,0:T(8,128)S(1)}, f32[192,768]{1,0:T(8,128)}, u32[]{:S(2)}) copy-start(f32[192,768]{1,0:T(8,128)} %param.20) | copy-start | bytes 1769476
  356.2 202.9 %copy-start.6 = (f32[192,768]{1,0:T(8,128)S(1)}, f32[192,768]{1,0:T(8,128)}, u32[]{:S(2)}) copy-start(f32[192,768]{1,0:T(8,128)} %param.21) | copy-start | bytes 1769476
  356.2 202.9 %copy-start.7 = (f32[192,768]{1,0:T(8,128)S(1)}, f32[192,768]{1,0:T(8,128)}, u32[]{:S(2)}) copy-start(f32[192,768]{1,0:T(8,128)} %param.22) | copy-start | bytes 1769476
Sparse Core Ops, SparseCore 0:
  11.4 66.3 all-gather.3
  81.1 80.1 all-gather.5
  311.8 106.2 reduce-scatter.3
  423.8 135.1 reduce-scatter.5
